TPU v7x, 64 devices: a 2x2x8 block of a 4x4x8 slice. The times are simulated.
64 devices in a mesh: data: 4 (over x, y), sp: 16 (over z, core).
Axes of the slice: x: 2, y: 2, z: 8, core: 2. Of those that a mesh axis runs over, the one named last changes fastest.
The devices are a block of a 4x4x8 slice.
Arguments:
- latent: bfloat16 [4, 96, 768, 1152], P('data', 'sp'), parts along dimension 0
- ln_gain: bfloat16 [4, 1152], replicated
- ln_bias: bfloat16 [4, 1152], replicated
- w_qkv: bfloat16 [2, 1152, 3, 16, 72], replicated
- w_out: bfloat16 [2, 16, 72, 1152], replicated
- w_up: bfloat16 [2, 1152, 4608], replicated
- w_down: bfloat16 [2, 4608, 1152], replicated
Outputs:
- output: bfloat16 [4, 96, 768, 1152], P('data', 'sp'), parts along dimension 0
There are 4 independent parts. A program takes and returns all parts, laid end to end along the dimension named above; an argument that names none is the same for every part.
All inputs are finite; a program needn't handle non-finite values.
Results may differ from a plain program's by a relative error of at most 0.0125955.
Values are sent between devices in bfloat16 or wider.
A program may use at most 768 MiB of HBM per device.

v0:
```python
import jax
import jax.numpy as jnp
from jax import lax
from jax.sharding import PartitionSpec as P, NamedSharding

LN_EPS = 1e-6
SPACE_FORMS = ('btqhk,btphk->bthqp', 'bthqp,btphk->btqhk')
TIME_FORMS = ('bqshk,bpshk->bshqp', 'bshqp,bpshk->bqshk')


def layer_norm(tokens, gain_vec, shift_vec):
    as_float = tokens.astype(jnp.float32)
    mean_val = jnp.mean(as_float, axis=-1, keepdims=True)
    centered = as_float - mean_val
    variance = jnp.mean(centered * centered, axis=-1, keepdims=True)
    normed = centered * lax.rsqrt(variance + LN_EPS) * gain_vec.astype(jnp.float32) + shift_vec.astype(jnp.float32)
    return normed.astype(jnp.bfloat16)


def project_qkv(tokens, gain_vec, shift_vec, w_qkv_blk):
    normed = layer_norm(tokens, gain_vec, shift_vec)
    return jnp.einsum('btsd,dchk->btschk', normed, w_qkv_blk, preferred_element_type=jnp.float32).astype(jnp.bfloat16)


def attend(qkv_all, ein_forms):
    score_scale = qkv_all.shape[-1] ** -0.5
    query_rows = qkv_all[:, :, :, 0]
    key_rows = qkv_all[:, :, :, 1]
    value_rows = qkv_all[:, :, :, 2]
    scores = jnp.einsum(ein_forms[0], query_rows, key_rows, preferred_element_type=jnp.float32) * score_scale
    attn_probs = jax.nn.softmax(scores, axis=-1).astype(jnp.bfloat16)
    return jnp.einsum(ein_forms[1], attn_probs, value_rows, preferred_element_type=jnp.float32).astype(jnp.bfloat16)


def finish_block(tokens, attended, gain_vec, shift_vec, w_out_blk, w_up_blk, w_down_blk):
    projected = jnp.einsum('btshk,hkd->btsd', attended, w_out_blk, preferred_element_type=jnp.float32)
    residual = (tokens.astype(jnp.float32) + projected).astype(jnp.bfloat16)
    normed = layer_norm(residual, gain_vec, shift_vec)
    hidden = jax.nn.gelu(jnp.einsum('btsd,df->btsf', normed, w_up_blk, preferred_element_type=jnp.float32), approximate=True).astype(jnp.bfloat16)
    result = residual.astype(jnp.float32) + jnp.einsum('btsf,fd->btsd', hidden, w_down_blk, preferred_element_type=jnp.float32)
    return result.astype(jnp.bfloat16)


def value_a9(tokens, layer_idx, ein_forms, ln_gain, ln_bias, w_qkv, w_out, w_up, w_down):
    qkv_all = project_qkv(tokens, ln_gain[2 * layer_idx], ln_bias[2 * layer_idx], w_qkv[layer_idx])
    attended = attend(qkv_all, ein_forms)
    return finish_block(tokens, attended, ln_gain[2 * layer_idx + 1], ln_bias[2 * layer_idx + 1], w_out[layer_idx], w_up[layer_idx], w_down[layer_idx])


def solution(mesh):
    act_spec = P('data', 'sp', None, None)

    def local_run(local_latent, ln_gain, ln_bias, w_qkv, w_out, w_up, w_down):
        mixed_act = value_a9(local_latent, 0, SPACE_FORMS, ln_gain, ln_bias, w_qkv, w_out, w_up, w_down)
        mixed_act = lax.all_to_all(mixed_act, 'sp', 2, 1, tiled=True)
        mixed_act = value_a9(mixed_act, 1, TIME_FORMS, ln_gain, ln_bias, w_qkv, w_out, w_up, w_down)
        return lax.all_to_all(mixed_act, 'sp', 1, 2, tiled=True)

    return jax.shard_map(local_run, mesh=mesh, in_specs=(act_spec, P(), P(), P(), P(), P(), P()), out_specs=act_spec, check_vma=False)
```

profile of v0, /device:TPU:21, one launch (start us, length us, event | category | flops | bytes accessed | tf_op | source)
XLA Modules:
  0.0 1462.8 jit_solution(5619321052021932152)
XLA Ops:
  0.0 0.0 copy-start.1
  0.0 0.0 copy-start.2
  0.0 5.5 convert_reduce_fusion.2
  5.5 7.0 fusion.43
  12.5 0.0 copy-done.1
  12.6 0.0 copy-done.2
  12.6 0.7 convert_reduce_fusion.3
  13.3 51.3 %convert_bitcast_fusion.1 = bf16[1,6,768,3,16,72]{2,5,4,3,1,0:T(8,128)(2,1)} fusion(bf16[1,6,768,1152]{3,2,1,0:T(8,128)(2,1)} %param.7, f32[1152]{0:T(1024)S(1)} %get-tuple-element.11, f32[1152]{0:T(1024)S(1)} %get-tuple-element.25, f32[6,768]{1,0:T(8,128)S(1)} %add_rsqrt_fusion.3, f32[6,768]{1,0:T(8,128)S(1)} %broadcast_multiply_fusion.3, ...), kind=kOutput, calls=%fused_computation.39 | convolution fusion | flops 36739547136 | bytes 50476032 | tf_op jit(solution)/shard_map/btsd,dchk->btschk/dot_general | solution.py:22
  64.6 84.4 %fusion.121 = (f32[6,16,768]{2,1,0:T(8,128)S(1)}, f32[6,16,768,768]{2,3,1,0:T(8,128)}) fusion(bf16[1,6,768,3,16,72]{2,5,4,3,1,0:T(8,128)(2,1)} %convert_bitcast_fusion.1), kind=kOutput, calls=%fused_computation.143 | convolution fusion | flops 8323596800 | bytes 248020992 | tf_op jit(solution)/shard_map/sub | solution.py:31
  149.0 75.4 %fusion.66.clone.5 = bf16[6,768,16,72]{1,3,2,0:T(8,128)(2,1)} fusion(f32[6,16,768,768]{2,3,1,0:T(8,128)} %get-tuple-element.19, f32[6,16,768]{2,1,0:T(8,128)S(1)} %get-tuple-element.18, bf16[1,6,768,3,16,72]{2,5,4,3,1,0:T(8,128)(2,1)} %convert_bitcast_fusion.1), kind=kOutput, calls=%fused_computation.86.clone.clone.clone.2 | convolution fusion | flops 8272281600 | bytes 248020992 | tf_op jit(solution)/shard_map/bthqp,btphk->btqhk/dot_general | solution.py:32
  224.4 0.0 copy-start.7
  224.4 0.0 copy-start.8
  224.4 22.9 %convert_reduce_fusion.1 = (f32[6,768]{1,0:T(8,128)S(1)}, bf16[1,6,768,1152]{3,2,1,0:T(8,128)(2,1)}) fusion(bf16[2,16,72,1152]{3,2,1,0:T(8,128)(2,1)} %param.11, bf16[1,6,768,1152]{3,2,1,0:T(8,128)(2,1)} %param.7, bf16[6,768,16,72]{1,3,2,0:T(8,128)(2,1)} %fusion.66.clone.5), kind=kOutput, calls=%fused_computation.38 | convolution fusion | flops 12257128448 | bytes 34523136 | tf_op jit(solution)/shard_map/btshk,hkd->btsd/dot_general | solution.py:36
  247.2 7.0 fusion.39
  254.3 0.0 copy-done.7
  254.3 0.0 copy-done.8
  254.3 76.5 %fusion.14.clone.7 = bf16[6,768,4608]{2,1,0:T(8,128)(2,1)} fusion(bf16[1,6,768,1152]{3,2,1,0:T(8,128)(2,1)} %get-tuple-element.21, bf16[2,1152,4608]{2,1,0:T(8,128)(2,1)} %param.12, f32[1152]{0:T(1024)S(1)} %copy-done.7, f32[1152]{0:T(1024)S(1)} %copy-done.8, f32[6,768]{1,0:T(8,128)S(1)} %add_rsqrt_fusion.2, ...), kind=kOutput, calls=%fused_computation.17.clone.clone.clone.clone.clone.2 | convolution fusion | flops 49145315328 | bytes 63747072 | tf_op jit(solution)/shard_map/btsd,df->btsf/dot_general | solution.py:39
  330.7 63.9 %fusion.48 = bf16[1,6,768,1152]{3,2,1,0:T(8,128)(2,1)} fusion(bf16[1,6,768,1152]{3,2,1,0:T(8,128)(2,1)} %get-tuple-element.21, bf16[2,4608,1152]{2,1,0:T(8,128)(2,1)} %param.13, bf16[6,768,4608]{2,1,0:T(8,128)(2,1)} %fusion.14.clone.7), kind=kOutput, calls=%fused_computation.62 | convolution fusion | flops 48938287104 | bytes 74317824 | tf_op jit(solution)/shard_map/btsf,fd->btsd/dot_general | solution.py:40
  394.7 16.3 %copy.18 = bf16[1,6,768,1152]{3,1,0,2:T(8,128)(2,1)S(1)} copy(bf16[1,6,768,1152]{3,2,1,0:T(8,128)(2,1)} %fusion.48) | data formatting | bytes 21233664 | tf_op jit(solution)/shard_map/convert_element_type | solution.py:41
  411.0 320.0 %all_to_all.27 = bf16[1,6,768,1152]{3,1,0,2:T(8,128)(2,1)S(1)} all-to-all(bf16[1,6,768,1152]{3,1,0,2:T(8,128)(2,1)S(1)} %copy.18), channel_id=1, replica_groups=mesh['data'=4,'sp'=16] {'sp'}, dimensions={2} | all-to-all | bytes 21233664 | tf_op jit(solution)/shard_map/all_to_all | solution.py:55
  731.0 0.0 copy-start.3
  731.0 0.0 copy-start.4
  731.0 3.3 bitcast_reduce_fusion
  734.3 0.0 copy-start
  734.3 3.0 multiply_reduce_fusion.2
  737.4 0.0 copy-done.3
  737.4 0.0 copy-done.4
  737.4 3.9 add_convert_fusion
  741.3 0.1 copy-done
  741.4 79.5 %convert_bitcast_fusion = bf16[1,96,48,3,16,72]{5,2,4,3,1,0:T(8,128)(2,1)} fusion(bf16[96,48,1152,1,1]{2,1,4,3,0:T(8,128)(2,1)S(1)} %bitcast.185, bf16[2,1152,3,16,72]{1,4,3,2,0:T(8,128)(2,1)} %param.10), kind=kOutput, calls=%fused_computation.27 | convolution fusion | flops 36707696640 | bytes 50429952 | tf_op jit(solution)/shard_map/btsd,dchk->btschk/dot_general | solution.py:22
  820.9 45.0 %slice_bitcast_fusion.2 = (bf16[96,48,16,72]{3,1,2,0:T(8,128)(2,1)}, bf16[96,48,16,72]{3,1,2,0:T(8,128)(2,1)}, bf16[96,48,16,72]{3,1,2,0:T(8,128)(2,1)}) fusion(bf16[1,96,48,3,16,72]{5,2,4,3,1,0:T(8,128)(2,1)} %convert_bitcast_fusion), kind=kLoop, calls=%fused_computation.70 | loop fusion | bytes 63700992 | tf_op jit(solution)/shard_map/reshape.35
  865.8 67.0 %fusion.51 = f32[48,16,96,96]{2,3,1,0:T(8,128)} fusion(bf16[96,48,16,72]{3,1,2,0:T(8,128)(2,1)} %get-tuple-element.16, bf16[96,48,16,72]{3,1,2,0:T(8,128)(2,1)} %get-tuple-element.17), kind=kOutput, calls=%fused_computation.73 | convolution fusion | flops 1019215872 | bytes 49545216 | tf_op jit(solution)/shard_map/bqshk,bpshk->bshqp/dot_general | solution.py:30
  932.9 42.3 %fusion.122 = (f32[48,16,96]{2,1,0:T(8,128)S(1)}, f32[48,16,96,96]{2,3,1,0:T(8,128)}) fusion(f32[48,16,96,96]{2,3,1,0:T(8,128)} %fusion.51), kind=kOutput, calls=%fused_computation.144 | output fusion | flops 28311648 | bytes 56918016 | tf_op jit(solution)/shard_map/sub | solution.py:31
  975.1 37.8 %convert_bitcast_fusion.2 = bf16[96,48,16,72]{0,3,2,1:T(8,128)(2,1)} fusion(f32[48,16,96,96]{2,3,1,0:T(8,128)} %get-tuple-element.23, f32[48,16,96]{2,1,0:T(8,128)S(1)} %get-tuple-element.22, bf16[96,48,16,72]{3,1,2,0:T(8,128)(2,1)} %get-tuple-element.15), kind=kOutput, calls=%fused_computation.77 | convolution fusion | flops 1038680064 | bytes 49840128 | tf_op jit(solution)/shard_map/bshqp,bpshk->bqshk/dot_general | solution.py:32
  1012.9 30.9 %copy.24 = bf16[96,48,16,72]{3,1,2,0:T(8,128)(2,1)} copy(bf16[96,48,16,72]{0,3,2,1:T(8,128)(2,1)} %convert_bitcast_fusion.2) | data formatting | bytes 21233664 | tf_op jit(solution)/shard_map/reshape.38
  1043.9 24.7 %fusion.55 = bf16[96,48,1152]{2,1,0:T(8,128)(2,1)} fusion(bf16[96,48,16,72]{3,1,2,0:T(8,128)(2,1)} %copy.24, f32[1,6,16,48,1152]{4,3,1,2,0:T(8,128)} %copy-done, bf16[2,16,72,1152]{3,2,1,0:T(8,128)(2,1)} %param.11), kind=kOutput, calls=%fused_computation.78 | convolution fusion | flops 12241207296 | bytes 53379072 | tf_op jit(solution)/shard_map/btshk,hkd->btsd/dot_general | solution.py:36
  1068.6 0.0 copy-start.5
  1068.6 0.0 copy-start.6
  1068.6 5.5 convert_reduce_fusion
  1074.1 7.0 fusion.35
  1081.1 0.0 copy-done.5
  1081.1 0.0 copy-done.6
  1081.1 76.4 %fusion.22.clone.5 = bf16[96,48,4608]{2,1,0:T(8,128)(2,1)} fusion(bf16[96,48,1152]{2,1,0:T(8,128)(2,1)} %fusion.55, bf16[2,1152,4608]{2,1,0:T(8,128)(2,1)} %param.12, f32[1152]{0:T(1024)S(1)} %copy-done.5, f32[1152]{0:T(1024)S(1)} %copy-done.6, f32[96,48]{1,0:T(8,128)S(1)} %add_rsqrt_fusion.1, f32[96,48]{1,0:T(8,128)S(1)} %broadcast_multiply_fusion.1), kind=kOutput, calls=%fused_computation.25.clone.clone.clone.2 | convolution fusion | flops 49145315328 | bytes 63747072 | tf_op jit(solution)/shard_map/btsd,df->btsf/dot_general | solution.py:39
  1157.5 63.8 %fusion.57 = bf16[1,96,48,1152]{3,2,0,1:T(8,128)(2,1)} fusion(bf16[96,48,1152]{2,1,0:T(8,128)(2,1)} %fusion.55, bf16[2,4608,1152]{2,1,0:T(8,128)(2,1)} %param.13, bf16[96,48,4608]{2,1,0:T(8,128)(2,1)} %fusion.22.clone.5), kind=kOutput, calls=%fused_computation.80 | convolution fusion | flops 48938287104 | bytes 74317824 | tf_op jit(solution)/shard_map/btsf,fd->btsd/dot_general | solution.py:40
  1221.4 236.6 %all_to_all.28 = bf16[1,96,48,1152]{3,2,0,1:T(8,128)(2,1)S(1)} all-to-all(bf16[1,96,48,1152]{3,2,0,1:T(8,128)(2,1)} %fusion.57), channel_id=1, replica_groups=mesh['data'=4,'sp'=16] {'sp'}, dimensions={1} | all-to-all | bytes 21233664 | tf_op jit(solution)/shard_map/all_to_all | solution.py:57
  1458.0 4.6 copy.26
  (8 shorter events, 0.1 us)
Async XLA Ops:
  0.0 12.5 copy-start.1
  0.0 12.6 copy-start.2
  224.4 29.9 %copy-start.7 = (f32[1152]{0:T(1024)S(1)}, f32[1152]{0:T(1024)}, u32[]{:S(2)}) copy-start(f32[1152]{0:T(1024)} %get-tuple-element.10) | copy-start | bytes 13828
  224.4 29.9 %copy-start.8 = (f32[1152]{0:T(1024)S(1)}, f32[1152]{0:T(1024)}, u32[]{:S(2)}) copy-start(f32[1152]{0:T(1024)} %get-tuple-element.26) | copy-start | bytes 13828
  731.0 6.4 copy-start.3
  731.0 6.4 copy-start.4
  734.3 7.1 copy-start
  1068.6 12.5 copy-start.5
  1068.6 12.5 copy-start.6
where the time goes:
time: 1470 us; the launch traced here: 1460 us
  matrix products  724 us (49%)
  blocking collectives  557 us (38%)
  local copies, waits for them, and re-layouts  96.9 us (7%)
  other arithmetic  85.2 us (6%)
    all_to_all x1, blocking collectives, local_run(): mixed_act = lax.all_to_all(mixed_act, 'sp', 2, 1, tiled=True)  320 us
    all_to_all x1, blocking collectives, local_run(): return lax.all_to_all(mixed_act, 'sp', 1, 2, tiled=True)  237 us
    dot_general x2, matrix products, finish_block(): jnp.einsum('btsd,df->btsf', normed, w_up_blk, preferred_element_type=jnp....  153 us
    dot_general x2, matrix products, project_qkv(): jnp.einsum('btsd,dchk->btschk', normed, w_qkv_blk, preferred_element_type...  131 us
    dot_general x2, matrix products, finish_block(): jnp.einsum('btsf,fd->btsd', hidden, w_down_blk, preferred_element_type=jn...  128 us
    dot_general x2, matrix products, attend(): jnp.einsum(ein_forms[1], attn_probs, value_rows, preferred_element_type=j...  113 us
    sub x1, matrix products, attend(): attn_probs = jax.nn.softmax(scores, axis=-1).astype(jnp.bfloat16)  84.4 us
    another operation x2, local copies, waits for them, and re-layouts  75.9 us

commit v1 on v0

v1 whole, which is shorter than its diff:
```python
import functools

import jax
import jax.numpy as jnp
from jax import lax
from jax.experimental import pallas as pl
from jax.experimental.pallas import tpu as pltpu
from jax.sharding import PartitionSpec as P

F32 = jnp.float32
BF16 = jnp.bfloat16
MESH = pl.DeviceIdType.MESH
LN_EPS = 1e-6
LOG2E = 1.4426950408889634
GROUP = 16
LANES = 8
QB = 256
KB = 128
RB = 32
UPB = 512
SLOTS = 3


def normalize(rows, gain, shift):
    inv = 1.0 / rows.shape[-1]
    cent = rows - jnp.sum(rows, axis=-1, keepdims=True) * inv
    var = jnp.sum(cent * cent, axis=-1, keepdims=True) * inv
    return (cent * lax.rsqrt(var + LN_EPS) * gain + shift).astype(BF16)


def gelu(x):
    c = 0.7978845608028654
    half = 0.5 * x
    return half + half * jnp.tanh(x * (c + (c * 0.044715) * (x * x)))


def fold(t, op):
    acc = t[0:8]
    for r in range(8, t.shape[0], 8):
        acc = op(acc, t[r:r + 8])
    return acc


def aligned(i, step):
    return pl.ds(pl.multiple_of(i * step, step), step)


def block_kernel(cfg, x_hbm, gain_ref, bias_ref, wqkv_hbm, wout_hbm, wup_hbm, wdown_hbm, y_hbm,
                 wqkv, wout, wup, wdown, xin, a, qkvt, ot, h, nb, u, y, s0, s1, p0, p1, m0, m1, l0, l1,
                 wsem, xsem, send_sem, recv_sem, own_sem):
    layer, temporal, n, units, tok, heads, hd = cfg
    width = heads * hd
    ff = wup.shape[1]
    per = tok // n
    tiles = per // GROUP
    rows = n * GROUP
    sbuf, pbuf, mbuf, lbuf = (s0, s1), (p0, p1), (m0, m1), (l0, l1)
    cscale = (hd ** -0.5) * LOG2E
    me = lax.axis_index('sp')

    def xcopy(unit, slot):
        src = x_hbm.at[:, aligned(unit, LANES), :] if temporal else x_hbm.at[unit]
        return pltpu.make_async_copy(src, xin.at[slot], xsem.at[slot])

    wcopies = [pltpu.make_async_copy(src.at[layer], dst, wsem.at[i]) for i, (src, dst) in enumerate(
        ((wqkv_hbm, wqkv), (wout_hbm, wout), (wup_hbm, wup), (wdown_hbm, wdown)))]
    xcopy(0, 0).start()
    for c in wcopies:
        c.start()

    barrier = pltpu.get_barrier_semaphore()
    for k in range(1, n):
        pl.semaphore_signal(barrier, inc=1, device_id={'sp': lax.rem(me + k, n)}, device_id_type=MESH)

    def target(unit, t):
        if temporal:
            return y_hbm.at[pl.ds(2 * t, 2), pl.ds(pl.multiple_of(me * (units * LANES) + unit * LANES, LANES), LANES), :]
        return y_hbm.at[me * units + unit, aligned(t, GROUP), :]

    def send(unit, t, slot, k):
        d = lax.rem(me + k, n)
        return pltpu.make_async_remote_copy(
            src_ref=y.at[slot, d], dst_ref=target(unit, t), send_sem=send_sem.at[slot], recv_sem=recv_sem,
            device_id={'sp': d}, device_id_type=MESH)

    def keep(unit, t, slot):
        return pltpu.make_async_copy(y.at[slot, me], target(unit, t), own_sem.at[slot])

    def drain(slot):
        keep(0, 0, slot).wait()
        whole = y.at[slot, pl.ds(0, n - 1)]
        pltpu.make_async_copy(whole, whole, send_sem.at[slot]).wait()

    def load_x(slot, block):
        if temporal:
            return xin[slot, aligned(block, QB // LANES)].reshape(QB, width).astype(F32)
        return xin[slot, aligned(block, QB), :].astype(F32)

    gains = [gain_ref[2 * layer + i:2 * layer + i + 1, :].astype(F32) for i in range(2)]
    shifts = [bias_ref[2 * layer + i:2 * layer + i + 1, :].astype(F32) for i in range(2)]

    def pre_norm(slot, block):
        a[aligned(block, QB), :] = normalize(load_x(slot, block), gains[0], shifts[0])

    nq, nk = tok // QB, tok // KB
    cols = [slice(b * QB, (b + 1) * QB) for b in range(nq)]

    def score(hh, par, c):
        k = qkvt[heads + hh, :, c * KB:(c + 1) * KB]
        for b in range(nq):
            s = lax.dot_general(k, qkvt[hh, :, cols[b]], (((0,), (0,)), ((), ())), preferred_element_type=F32)
            if temporal:
                row = lax.broadcasted_iota(jnp.int32, s.shape, 0)
                col = lax.broadcasted_iota(jnp.int32, s.shape, 1)
                s = jnp.where((row & (LANES - 1)) == (col & (LANES - 1)), s, -1e38)
            sbuf[par][c * KB:(c + 1) * KB, cols[b]] = s
            yield fold(s, jnp.maximum)

    def soften(par, ms, c):
        for b in range(nq):
            l = None
            for r in range(c * KB, (c + 1) * KB, RB):
                e = jnp.exp2((sbuf[par][r:r + RB, cols[b]] - ms[b]) * cscale)
                pbuf[par][r:r + RB, cols[b]] = e.astype(BF16)
                f = fold(e, jnp.add)
                l = f if l is None else l + f
            yield l

    def mix(hh, par, b):
        o = jnp.dot(qkvt[2 * heads + hh], pbuf[par][:, cols[b]], preferred_element_type=F32)
        ot[pl.ds(pl.multiple_of(hh * hd, 8), hd), cols[b]] = o * lbuf[par][:, cols[b]]

    def attend(hs, hm, j):
        ms = [jnp.max(mbuf[j][:, cl], axis=0, keepdims=True) for cl in cols]
        mx = ls = None
        for c in range(nk):
            fm, fl = [], []
            for x, z in zip(score(hs, 1 - j, c), soften(j, ms, c)):
                fm.append(x)
                fl.append(z)
            mx = fm if mx is None else [jnp.maximum(p, q) for p, q in zip(mx, fm)]
            ls = fl if ls is None else [p + q for p, q in zip(ls, fl)]
            if (c + 1) % (nk // nq) == 0:
                mix(hm, 1 - j, (c + 1) // (nk // nq) - 1)
        for b in range(nq):
            mbuf[1 - j][:, cols[b]] = mx[b]
            lbuf[j][:, cols[b]] = 1.0 / jnp.sum(ls[b], axis=0, keepdims=True)

    def unit_body(unit, _):
        slot = lax.rem(unit, 2)

        @pl.when(unit == 0)
        def _():
            xcopy(0, 0).wait()
            for b in range(nq):
                pre_norm(0, b)
            wcopies[0].wait()

        @pl.when(unit + 1 < units)
        def _():
            xcopy(unit + 1, 1 - slot).start()

        def qkv_body(i, _):
            r = lax.dot_general(wqkv[aligned(i, width), :], a[...], (((1,), (1,)), ((), ())), preferred_element_type=F32)
            qkvt[pl.ds(heads * i, heads)] = r.reshape(heads, hd, tok).astype(BF16)
            return 0
        lax.fori_loop(0, 3, qkv_body, 0)

        first = None
        for c in range(nk):
            fm = list(score(0, 0, c))
            first = fm if first is None else [jnp.maximum(p, q) for p, q in zip(first, fm)]
        for b in range(nq):
            mbuf[0][:, cols[b]] = first[b]

        def attn_body(i, _):
            def part(j):
                hh = 2 * i + j
                attend(jnp.minimum(hh + 1, heads - 1), jnp.maximum(hh - 1, 0), j)
            part(0)

            @pl.when(i < heads)
            def _():
                part(1)
            return 0
        lax.fori_loop(0, heads // 2, attn_body, 0)

        @pl.when(unit == 0)
        def _():
            wcopies[1].wait()

        for b in range(nq):
            mix(heads - 1, 1, b)
            p = lax.dot_general(ot[:, cols[b]].astype(BF16), wout[...], (((0,), (0,)), ((), ())),
                                preferred_element_type=F32)
            hv = (load_x(slot, b) + p).astype(BF16)
            g = QB // GROUP
            h[b * g:(b + 1) * g] = hv.reshape(g, GROUP, width)
            nb[b * g:(b + 1) * g] = normalize(hv.astype(F32), gains[1], shifts[1]).reshape(g, GROUP, width)

        @pl.when(unit == 0)
        def _():
            wcopies[2].wait()
            wcopies[3].wait()
            pl.semaphore_wait(barrier, n - 1)

        @pl.when(unit + 1 < units)
        def _():
            xcopy(unit + 1, 1 - slot).wait()

        def mlp_body(t, _):
            step = unit * tiles + t
            ys = lax.rem(step, SLOTS)

            @pl.when(step >= SLOTS)
            def _():
                drain(ys)
            hb = jnp.concatenate([h[d * tiles + t] for d in range(n)])
            nbt = jnp.concatenate([nb[d * tiles + t] for d in range(n)])
            for c in range(0, ff, UPB):
                u[:, c:c + UPB] = gelu(jnp.dot(nbt, wup[:, c:c + UPB], preferred_element_type=F32)).astype(BF16)
            cut = ff - UPB
            r = jnp.dot(u[:, :cut], wdown[:cut, :], preferred_element_type=F32)
            r = r + jnp.dot(u[:, cut:], wdown[cut:, :], preferred_element_type=F32)
            y[ys] = (hb.astype(F32) + r).astype(BF16).reshape(y.shape[1:])
            pre_norm(1 - slot, t)
            for k in range(1, n):
                send(unit, t, ys, k).start()
            keep(unit, t, ys).start()
            return 0
        lax.fori_loop(0, tiles, mlp_body, 0)
        return 0

    lax.fori_loop(0, units, unit_body, 0)
    for s in range(SLOTS):
        drain(s)
    if temporal:
        got = y_hbm.at[:, pl.ds(0, (n - 1) * units * LANES), :]
    else:
        got = y_hbm.at[pl.ds(0, (n - 1) * units)]
    pltpu.make_async_copy(got, got, recv_sem).wait()


def run_block(layer, temporal, n, heads, hd, x, gain, bias, wqkv, wout, wup, wdown):
    width = heads * hd
    ff = wup.shape[-1]
    if temporal:
        frames, per, _ = x.shape
        units, tok = per // LANES, frames * LANES
        out = jax.ShapeDtypeStruct((frames // n, per * n, width), BF16)
        xs, ys = (2, frames, LANES, width), (SLOTS, n, GROUP // LANES, LANES, width)
    else:
        units, tok, _ = x.shape
        out = jax.ShapeDtypeStruct((units * n, tok // n, width), BF16)
        xs, ys = (2, tok, width), (SLOTS, n, GROUP, width)
    anyspec = pl.BlockSpec(memory_space=pl.ANY)
    vspec = pl.BlockSpec(memory_space=pltpu.VMEM)
    sent = units * tok * width * 2
    return pl.pallas_call(
        functools.partial(block_kernel, (layer, temporal, n, units, tok, heads, hd)),
        out_shape=out,
        in_specs=[anyspec, vspec, vspec] + [anyspec] * 4,
        out_specs=anyspec,
        scratch_shapes=[
            pltpu.VMEM((3 * width, width), BF16), pltpu.VMEM((width, width), BF16),
            pltpu.VMEM((width, ff), BF16), pltpu.VMEM((ff, width), BF16),
            pltpu.VMEM(xs, BF16), pltpu.VMEM((tok, width), BF16),
            pltpu.VMEM((3 * heads, hd, tok), BF16), pltpu.VMEM((width, tok), F32),
            pltpu.VMEM((tok // GROUP, GROUP, width), BF16), pltpu.VMEM((tok // GROUP, GROUP, width), BF16),
            pltpu.VMEM((n * GROUP, ff), BF16), pltpu.VMEM(ys, BF16),
            pltpu.VMEM((tok, tok), F32), pltpu.VMEM((tok, tok), F32),
            pltpu.VMEM((tok, tok), BF16), pltpu.VMEM((tok, tok), BF16),
            pltpu.VMEM((8, tok), F32), pltpu.VMEM((8, tok), F32),
            pltpu.VMEM((1, tok), F32), pltpu.VMEM((1, tok), F32),
            pltpu.SemaphoreType.DMA((4,)), pltpu.SemaphoreType.DMA((2,)), pltpu.SemaphoreType.DMA((SLOTS,)),
            pltpu.SemaphoreType.DMA, pltpu.SemaphoreType.DMA((SLOTS,)),
        ],
        compiler_params=pltpu.CompilerParams(
            vmem_limit_bytes=67043328, collective_id=layer, has_side_effects=True),
        cost_estimate=pl.CostEstimate(flops=24 * units * tok * width * width, bytes_accessed=3 * sent, transcendentals=0),
        name=f'block{layer}',
    )(x, gain, bias, wqkv, wout, wup, wdown)


def solution(mesh):
    act_spec = P('data', 'sp', None, None)
    n = mesh.shape['sp']

    def local_run(x, gain, bias, w_qkv, w_out, w_up, w_down):
        layers, width, _, heads, hd = w_qkv.shape
        wqkvt = jnp.transpose(w_qkv, (0, 2, 3, 4, 1)).reshape(layers, 3 * width, width)
        wo = w_out.reshape(layers, width, width)
        y = run_block(0, False, n, heads, hd, x[0], gain, bias, wqkvt, wo, w_up, w_down)
        y = run_block(1, True, n, heads, hd, y, gain, bias, wqkvt, wo, w_up, w_down)
        return y[None]

    return jax.shard_map(local_run, mesh=mesh, in_specs=(act_spec,) + (P(),) * 6, out_specs=act_spec, check_vma=False)
```

time: 1470 us -> 624 us (0.42)
  matrix products: 724 us -> 0 us
  Pallas kernels: 0 us -> 615 us
  blocking collectives: 557 us -> 0 us
  local copies, waits for them, and re-layouts: 96.9 us -> 9.36 us
  other arithmetic: 85.2 us -> 0 us
    dot_general x11 -> x0, matrix products: 639 us -> none  [the longest x2 153 us: finish_block(): jnp.einsum('btsd,df->btsf', normed, w_up_blk, preferred_element_type=jnp....]
    pallas_call x0 -> x2, Pallas kernels: none -> 615 us  [run_block(): pl.pallas_call(functools.partial(block_kernel, (layer, temporal, n, units...]
    all_to_all x2 -> x0, blocking collectives: 557 us -> none  [the longest x1 320 us: local_run(): mixed_act = lax.all_to_all(mixed_act, 'sp', 2, 1, tiled=True)]
    sub x1 -> x0, matrix products: 84.4 us -> none  [attend(): attn_probs = jax.nn.softmax(scores, axis=-1).astype(jnp.bfloat16)]
    another operation x2 -> x0, local copies, waits for them, and re-layouts: 75.9 us -> none
    sub x1 -> x0, other arithmetic: 42.3 us -> none  [attend(): attn_probs = jax.nn.softmax(scores, axis=-1).astype(jnp.bfloat16)]
    reduce_sum x7 -> x0, other arithmetic: 38.2 us -> none  [the longest x4 24 us: layer_norm(): variance = jnp.mean(centered * centered, axis=-1, keepdims=True)]
    convert_element_type x1 -> x0, local copies, waits for them, and re-layouts: 16.3 us -> none  [finish_block(): return result.astype(jnp.bfloat16)]
where the time goes in v1:
time: 624 us
  Pallas kernels  615 us (99%)
  local copies, waits for them, and re-layouts  9.36 us (2%)
    pallas_call x2, Pallas kernels, run_block(): pl.pallas_call(functools.partial(block_kernel, (layer, temporal, n, units...  615 us

profile of v1, /device:TPU:21, one launch (start us, length us, event | category | flops | bytes accessed | tf_op | source)
XLA Modules:
  0.0 624.1 jit_solution(15778668147449507113)
XLA Ops:
  0.0 306.3 %block0.1.x_hbm = bf16[96,48,1152]{2,1,0:T(8,128)(2,1)} custom-call(bf16[6,768,1152]{2,1,0:T(8,128)(2,1)} %bitcast.9, bf16[4,1152]{1,0:T(4,128)(2,1)} %gain_ref.3, bf16[4,1152]{1,0:T(4,128)(2,1)} %bias_ref.3, bf16[2,3456,1152]{2,1,0:T(8,128)(2,1)} %bitcast.7, bf16[2,1152,1152]{2,1,0:T(8,128)(2,1)} %bitcast.10, bf16[2,1152,4608]{2,1,0:T(8,128)(2,1)} %wup_hbm.3, ...), custom_call_target="tpu_custom_call" | custom-call | flops 146767085568 | bytes 31850496 | tf_op jit(solution)/shard_map/block0/pallas_call | solution.py:259
  306.3 308.4 %block1.1 = bf16[6,768,1152]{2,1,0:T(8,128)(2,1)} custom-call(bf16[96,48,1152]{2,1,0:T(8,128)(2,1)} %block0.1.x_hbm, bf16[4,1152]{1,0:T(4,128)(2,1)} %gain_ref.3, bf16[4,1152]{1,0:T(4,128)(2,1)} %bias_ref.3, bf16[2,3456,1152]{2,1,0:T(8,128)(2,1)} %bitcast.8, bf16[2,1152,1152]{2,1,0:T(8,128)(2,1)} %bitcast.11, bf16[2,1152,4608]{2,1,0:T(8,128)(2,1)} %wup_hbm.3, ...), custom_call_target="tpu_custom_call" | custom-call | flops 146767085568 | bytes 31850496 | tf_op jit(solution)/shard_map/block1/pallas_call | solution.py:259
  614.7 9.4 %copy.9 = bf16[1,6,768,1152]{3,2,1,0:T(8,128)(2,1)} copy(bf16[1,6,768,1152]{3,2,1,0:T(8,128)(2,1)} %bitcast.6) | data formatting | bytes 21233664

commit v2 on v0

v2 whole, which is shorter than its diff:
```python
import functools

import jax
import jax.numpy as jnp
from jax import lax
from jax.experimental import pallas as pl
from jax.experimental.pallas import tpu as pltpu
from jax.sharding import PartitionSpec as P

F32 = jnp.float32
BF16 = jnp.bfloat16
MESH = pl.DeviceIdType.MESH
LN_EPS = 1e-6
LOG2E = 1.4426950408889634
SUB = 8
PAIR = 2
LANE = 128
QB = 256
KB = 128
RB = 32
UPB = 512
SLOTS = 3
NEG = -1e38


def normalize(rows, gain, shift):
    inv = 1.0 / rows.shape[-1]
    cent = rows - jnp.sum(rows, axis=-1, keepdims=True) * inv
    var = jnp.sum(cent * cent, axis=-1, keepdims=True) * inv
    return cent * lax.rsqrt(var + LN_EPS) * gain + shift


def gelu(x):
    c = 0.7978845608028654
    half = 0.5 * x
    return half + half * jnp.tanh(x * (c + (c * 0.044715) * (x * x)))


def fold(t, op):
    acc = t[0:8]
    for r in range(8, t.shape[0], 8):
        acc = op(acc, t[r:r + 8])
    return acc


def aligned(i, step):
    return pl.ds(pl.multiple_of(i * step, step), step)


def blocks_kernel(cfg, x_hbm, gain_ref, bias_ref, wqkv_hbm, wout_hbm, wup_hbm, wdown_hbm, out_hbm, mid_hbm,
                  wqkv, wout, wup, wdown, xin, xs, a, qkvt, ot, h, nb, nb2, u, y,
                  s0, s1, p0, p1, m0, m1, l0, l1, wsem, xsem, send_sem, own_sem, mid_sem, out_sem):
    n, heads, hd, space_units, time_units = cfg
    units = space_units + time_units
    width = heads * hd
    ff = wup.shape[1]
    tiles = xin.shape[1]
    rows = n * PAIR * SUB
    tok = tiles * rows
    frames = tok // SUB
    groups = rows // SUB
    lanes = width // LANE
    sbuf, pbuf, mbuf, lbuf = (s0, s1), (p0, p1), (m0, m1), (l0, l1)
    cscale = (hd ** -0.5) * LOG2E
    me = lax.axis_index('sp')

    def other(k):
        d = me + k
        return jnp.where(d >= n, d - n, d)

    def xfetch(unit, slot):
        @pl.when(unit < space_units)
        def _():
            for t in range(tiles):
                pltpu.make_async_copy(
                    x_hbm.at[unit, :, pl.ds(t * PAIR, PAIR)], xin.at[slot, t], xsem.at[slot]).start()

        @pl.when(unit >= space_units)
        def _():
            for t in range(tiles):
                pltpu.make_async_copy(
                    mid_hbm.at[:, pl.ds(t * PAIR, PAIR), unit - space_units], xin.at[slot, t], xsem.at[slot]).start()

    def xwait(slot):
        pltpu.make_async_copy(xin.at[slot], xin.at[slot], xsem.at[slot]).wait()

    def mid_wait(t):
        part = mid_hbm.at[pl.ds(0, n - 1), :, pl.ds(t * PAIR, PAIR)]
        pltpu.make_async_copy(part, part, mid_sem.at[t]).wait()

    def wcopy(i, layer):
        src = (wqkv_hbm, wout_hbm, wup_hbm, wdown_hbm)[i]
        return pltpu.make_async_copy(src.at[layer], (wqkv, wout, wup, wdown)[i], wsem.at[i])

    xfetch(0, 0)
    for i in range(4):
        wcopy(i, 0).start()

    barrier = pltpu.get_barrier_semaphore()
    for k in range(1, n):
        pl.semaphore_signal(barrier, inc=1, device_id={'sp': other(k)}, device_id_type=MESH)

    def send(temporal, unit, t, slot):
        if temporal:
            target, sem = out_hbm.at[pl.ds(t * PAIR, PAIR), me * time_units + (unit - space_units)], out_sem
        else:
            target, sem = mid_hbm.at[me, unit, pl.ds(t * PAIR, PAIR)], mid_sem.at[t]
        for k in range(1, n):
            d = other(k)
            pltpu.make_async_remote_copy(
                src_ref=y.at[slot, d], dst_ref=target, send_sem=send_sem.at[slot], recv_sem=sem,
                device_id={'sp': d}, device_id_type=MESH).start()
        pltpu.make_async_copy(y.at[slot, me], target, own_sem.at[slot]).start()

    def own_wait(slot):
        pltpu.make_async_copy(y.at[slot, 0], y.at[slot, 0], own_sem.at[slot]).wait()

    def send_wait(slot):
        whole = y.at[slot, pl.ds(0, n - 1)]
        pltpu.make_async_copy(whole, whole, send_sem.at[slot]).wait()

    gain_all, shift_all = gain_ref[...].astype(F32), bias_ref[...].astype(F32)

    def params(layer, i):
        pick = lambda p: jnp.where(layer > 0, p[2 + i:3 + i], p[i:i + 1])
        return pick(gain_all), pick(shift_all)

    def load_x(slot, t, r0, nr):
        step = PAIR * SUB
        return xin[slot, t, r0 // step:(r0 + nr) // step].reshape(nr, width).astype(F32)

    def pre_norm(temporal, slot, t, r0, nr, par):
        v = normalize(load_x(slot, t, r0, nr), *par)
        if temporal:
            for c in range(lanes):
                xs[c, r0:r0 + nr, :] = v[:, c * LANE:(c + 1) * LANE]
        else:
            a[pl.ds(pl.multiple_of(t * rows + r0, nr), nr), :] = v.astype(BF16)

    def spread(t, g0, ng):
        for p in range(SUB):
            at = pl.ds(pl.multiple_of(p * frames + t * groups + g0, ng), ng)
            for c in range(lanes):
                a[at, c * LANE:(c + 1) * LANE] = xs[c, pl.ds(g0 * SUB + p, ng, stride=SUB), :].astype(BF16)

    def held(c):
        per_buf = tok // LANE
        return sbuf[c // per_buf].at[c % per_buf]

    def mid_norm(temporal, dst, slot, t, r0, nr, par):
        if temporal:
            parts = []
            for g in range(r0 // SUB, (r0 + nr) // SUB):
                at = pl.ds(t * groups + g, SUB, stride=frames)
                parts.append(jnp.concatenate([held(c)[at, :] for c in range(lanes)], axis=1))
            h[t, r0:r0 + nr, :] = (load_x(slot, t, r0, nr) + jnp.concatenate(parts)).astype(BF16)
        dst[r0:r0 + nr, :] = normalize(h[t, r0:r0 + nr, :].astype(F32), *par).astype(BF16)

    nq, nk = tok // QB, tok // KB
    cols = [slice(b * QB, (b + 1) * QB) for b in range(nq)]

    def mix(hh, par, b):
        o = jnp.dot(qkvt[2 * heads + hh], pbuf[par][:, cols[b]], preferred_element_type=F32)
        ot[pl.ds(pl.multiple_of(hh * hd, 8), hd), cols[b]] = o * lbuf[par][:, cols[b]]

    def weigh(par, r0, nr, q, m):
        l = None
        for r in range(r0, r0 + nr, RB):
            e = jnp.exp2((sbuf[par][q // LANE, r:r + RB, :] - m) * cscale)
            pbuf[par][r:r + RB, q:q + LANE] = e.astype(BF16)
            f = fold(e, jnp.add)
            l = f if l is None else l + f
        return l

    def per_lane(b):
        return range(b * QB, (b + 1) * QB, LANE)

    def space_score(hh, par, c):
        k = qkvt[heads + hh, :, c * KB:(c + 1) * KB]
        for b in range(nq):
            s = lax.dot_general(k, qkvt[hh, :, cols[b]], (((0,), (0,)), ((), ())), preferred_element_type=F32)
            for q in per_lane(b):
                sbuf[par][q // LANE, c * KB:(c + 1) * KB, :] = s[:, q - b * QB:q - b * QB + LANE]
            yield fold(s, jnp.maximum)

    def space_first():
        first = None
        for c in range(nk):
            fm = list(space_score(0, 0, c))
            first = fm if first is None else [jnp.maximum(p, q) for p, q in zip(first, fm)]
        for b in range(nq):
            mbuf[0][:, cols[b]] = first[b]

    def space_attend(hs, hm, j):
        ms = [jnp.max(mbuf[j][:, cl], axis=0, keepdims=True) for cl in cols]
        mx = ls = None
        for c in range(nk):
            fm, fl = [], []
            for b, x in enumerate(space_score(hs, 1 - j, c)):
                fm.append(x)
                fl.append(jnp.concatenate(
                    [weigh(j, c * KB, KB, q, ms[b][:, q - b * QB:q - b * QB + LANE]) for q in per_lane(b)], axis=1))
            mx = fm if mx is None else [jnp.maximum(p, q) for p, q in zip(mx, fm)]
            ls = fl if ls is None else [p + q for p, q in zip(ls, fl)]
            if (c + 1) % (nk // nq) == 0:
                mix(hm, 1 - j, (c + 1) // (nk // nq) - 1)
        for b in range(nq):
            mbuf[1 - j][:, cols[b]] = mx[b]
            lbuf[j][:, cols[b]] = 1.0 / jnp.sum(ls[b], axis=0, keepdims=True)

    def span(lo, hi):
        return lo // frames * frames, -(-hi // frames) * frames

    def time_score(hh, par, b):
        kt = jnp.transpose(qkvt[heads + hh])
        lo, hi = span(b * QB, (b + 1) * QB)
        s = jnp.dot(kt[lo:hi], qkvt[hh, :, cols[b]], preferred_element_type=F32)
        for q in per_lane(b):
            mx = None
            k0, k1 = span(q, q + LANE)
            for r in range(k0, k1, frames):
                v = s[r - lo:r - lo + frames, q - b * QB:q - b * QB + LANE]
                lane = q + lax.broadcasted_iota(jnp.int32, v.shape, 1)
                v = jnp.where((lane >= r) & (lane < r + frames), v, NEG)
                sbuf[par][q // LANE, r:r + frames, :] = v
                f = fold(v, jnp.maximum)
                mx = f if mx is None else jnp.maximum(mx, f)
            mbuf[par][:, q:q + LANE] = mx

    def time_soften(par, b):
        for q in per_lane(b):
            k0, k1 = span(q, q + LANE)
            m = jnp.max(mbuf[par][:, q:q + LANE], axis=0, keepdims=True)
            l = weigh(par, k0, k1 - k0, q, m)
            lbuf[par][:, q:q + LANE] = 1.0 / jnp.sum(l, axis=0, keepdims=True)

    def time_first():
        for b in range(nq):
            time_score(0, 0, b)

    def time_attend(hs, hm, j):
        for b in range(nq):
            time_score(hs, 1 - j, b)
            time_soften(j, b)
            mix(hm, 1 - j, b)

    def attention(first, attend, split):
        first()

        def body(i, _):
            def part(j):
                hh = 2 * i + j
                attend(jnp.minimum(hh + 1, heads - 1), jnp.maximum(hh - 1, 0), j)
            part(0)
            if split:
                pl.when(i < heads)(functools.partial(part, 1))
            else:
                part(1)
            return 0
        lax.fori_loop(0, heads // 2, body, 0)

    def unit_body(unit, _):
        slot = lax.rem(unit, 2)
        layer = jnp.where(unit < space_units, 0, 1)
        opening = (unit == 0) | (unit == space_units)
        closing = unit == space_units - 1
        ahead = (unit + 1 < units) & (unit + 1 != space_units)

        def head(temporal):
            xwait(slot)
            par = params(layer, 0)

            def head_norm(t, _):
                pre_norm(temporal, slot, t, 0, rows, par)
                if temporal:
                    spread(t, 0, groups)
                return 0
            lax.fori_loop(0, tiles, head_norm, 0)
            wcopy(0, 0).wait()

        pl.when(unit == 0)(lambda: head(False))

        @pl.when(unit == space_units)
        def _():
            head(True)
            p0[...] = jnp.zeros_like(p0)
            p1[...] = jnp.zeros_like(p1)

        for t in range(1, tiles):
            pl.when(unit + 1 == space_units + t * PAIR)(functools.partial(mid_wait, t))

        @pl.when(ahead)
        def _():
            xfetch(unit + 1, 1 - slot)

        def qkv_body(i, _):
            r = lax.dot_general(wqkv[aligned(i, width), :], a[...], (((1,), (1,)), ((), ())), preferred_element_type=F32)
            qkvt[pl.ds(heads * i, heads)] = r.reshape(heads, hd, tok).astype(BF16)
            return 0
        lax.fori_loop(0, 3, qkv_body, 0)

        @pl.when(closing)
        def _():
            wcopy(0, 1).start()

        pl.when(layer == 0)(lambda: attention(space_first, space_attend, True))
        pl.when(layer == 1)(lambda: attention(time_first, time_attend, False))

        @pl.when(opening)
        def _():
            wcopy(1, 0).wait()

        par1 = params(layer, 1)

        def project(temporal):
            for b in range(nq):
                mix(heads - 1, 1, b)
                r = lax.dot_general(ot[:, cols[b]].astype(BF16), wout[...], (((0,), (0,)), ((), ())),
                                    preferred_element_type=F32)
                if temporal:
                    for c in range(lanes):
                        held(c)[cols[b], :] = r[:, c * LANE:(c + 1) * LANE]
                else:
                    h[b] = (load_x(slot, b, 0, rows) + r).astype(BF16)
                    if b == 0:
                        mid_norm(False, nb, slot, 0, 0, rows, par1)
            if temporal:
                mid_norm(True, nb, slot, 0, 0, rows, par1)

        pl.when(layer == 0)(lambda: project(False))
        pl.when(layer == 1)(lambda: project(True))

        @pl.when(closing)
        def _():
            wcopy(1, 1).start()

        @pl.when(opening)
        def _():
            wcopy(2, 0).wait()
            wcopy(3, 0).wait()

        @pl.when(unit == 0)
        def _():
            pl.semaphore_wait(barrier, n - 1)

        @pl.when(ahead)
        def _():
            xwait(1 - slot)

        par0 = params(layer, 0)
        steps = ff // UPB
        piece = -(-rows // steps // 32) * 32

        def mlp_body(temporal, t, _):
            step = unit * tiles + t
            ys = lax.rem(step, SLOTS)

            @pl.when(step >= SLOTS)
            def _():
                send_wait(ys)

            @pl.when((step >= SLOTS) & ((step < space_units * tiles) | (step >= space_units * tiles + SLOTS)))
            def _():
                own_wait(ys)

            after = jnp.minimum(t + 1, tiles - 1)
            half = rows // 2
            for i in range(steps):
                c = i * UPB
                u[:, c:c + UPB] = gelu(jnp.dot(nb[...], wup[:, c:c + UPB], preferred_element_type=F32)).astype(BF16)
                r0 = i * piece
                if r0 < rows:
                    mid_norm(temporal, nb2, slot, after, r0, piece, par1)
                    pre_norm(temporal, 1 - slot, t, r0, piece, par0)
                    if temporal and (r0 + piece) % half == 0:
                        spread(t, (r0 + piece - half) // SUB, half // SUB)
            cut = ff - UPB
            r = jnp.dot(u[:, :cut], wdown[:cut, :], preferred_element_type=F32)
            r = r + jnp.dot(u[:, cut:], wdown[cut:, :], preferred_element_type=F32)
            y[ys] = (h[t].astype(F32) + r).astype(BF16).reshape(y.shape[1:])
            nb[...] = nb2[...]
            send(temporal, unit, t, ys)
            return 0
        def mlp(temporal):
            lax.fori_loop(0, tiles, functools.partial(mlp_body, temporal), 0)

        for temporal in (False, True):
            pl.when(layer == int(temporal))(functools.partial(mlp, temporal))

        @pl.when(closing)
        def _():
            wcopy(2, 1).start()
            wcopy(3, 1).start()
            for s in range(SLOTS):
                own_wait(s)
            mid_wait(0)
            xfetch(unit + 1, 1 - slot)
        return 0

    lax.fori_loop(0, units, unit_body, 0)
    for s in range(SLOTS):
        send_wait(s)
        own_wait(s)
    got = out_hbm.at[:, pl.ds(0, (n - 1) * time_units)]
    pltpu.make_async_copy(got, got, out_sem).wait()


def run_blocks(n, heads, hd, x, gain, bias, wqkv, wout, wup, wdown):
    local, patches, width = x.shape
    ff = wup.shape[-1]
    per = patches // n // SUB
    x = x.reshape(local, n, per, SUB, width)
    rows = n * PAIR * SUB
    tok = patches
    tiles = tok // rows
    assert tok == n * local * SUB and tiles * PAIR == per == local
    anyspec = pl.BlockSpec(memory_space=pl.ANY)
    vspec = pl.BlockSpec(memory_space=pltpu.VMEM)
    sent = 2 * local * tok * width * 2
    out, _ = pl.pallas_call(
        functools.partial(blocks_kernel, (n, heads, hd, local, per)),
        out_shape=(jax.ShapeDtypeStruct((local, n * per, SUB, width), BF16),
                   jax.ShapeDtypeStruct((n, local, per, SUB, width), BF16)),
        in_specs=[anyspec, vspec, vspec] + [anyspec] * 4,
        out_specs=(anyspec, anyspec),
        scratch_shapes=[
            pltpu.VMEM((3 * width, width), BF16), pltpu.VMEM((width, width), BF16),
            pltpu.VMEM((width, ff), BF16), pltpu.VMEM((ff, width), BF16),
            pltpu.VMEM((2, tiles, n, PAIR, SUB, width), BF16), pltpu.VMEM((width // LANE, rows, LANE), F32),
            pltpu.VMEM((tok, width), BF16), pltpu.VMEM((3 * heads, hd, tok), BF16), pltpu.VMEM((width, tok), F32),
            pltpu.VMEM((tiles, rows, width), BF16), pltpu.VMEM((rows, width), BF16), pltpu.VMEM((rows, width), BF16),
            pltpu.VMEM((rows, ff), BF16), pltpu.VMEM((SLOTS, n, PAIR, SUB, width), BF16),
            pltpu.VMEM((tok // LANE, tok, LANE), F32), pltpu.VMEM((tok // LANE, tok, LANE), F32),
            pltpu.VMEM((tok, tok), BF16), pltpu.VMEM((tok, tok), BF16),
            pltpu.VMEM((8, tok), F32), pltpu.VMEM((8, tok), F32),
            pltpu.VMEM((1, tok), F32), pltpu.VMEM((1, tok), F32),
            pltpu.SemaphoreType.DMA((4,)), pltpu.SemaphoreType.DMA((2,)), pltpu.SemaphoreType.DMA((SLOTS,)),
            pltpu.SemaphoreType.DMA((SLOTS,)), pltpu.SemaphoreType.DMA((tiles,)), pltpu.SemaphoreType.DMA,
        ],
        compiler_params=pltpu.CompilerParams(
            vmem_limit_bytes=67043328, collective_id=0, has_side_effects=True),
        cost_estimate=pl.CostEstimate(flops=48 * local * tok * width * width, bytes_accessed=4 * sent, transcendentals=0),
        name='blocks',
    )(x, gain, bias, wqkv, wout, wup, wdown)
    return out.reshape(local, patches, width)


def solution(mesh):
    act_spec = P('data', 'sp', None, None)
    n = mesh.shape['sp']

    def local_run(x, gain, bias, w_qkv, w_out, w_up, w_down):
        layers, width, _, heads, hd = w_qkv.shape
        wqkvt = jnp.transpose(w_qkv, (0, 2, 3, 4, 1)).reshape(layers, 3 * width, width)
        wo = w_out.reshape(layers, width, width)
        return run_blocks(n, heads, hd, x[0], gain, bias, wqkvt, wo, w_up, w_down)[None]

    return jax.shard_map(local_run, mesh=mesh, in_specs=(act_spec,) + (P(),) * 6, out_specs=act_spec, check_vma=False)
```

time: 1470 us -> 594 us (0.40)
  matrix products: 724 us -> 0 us
  Pallas kernels: 0 us -> 584 us
  blocking collectives: 557 us -> 0 us
  local copies, waits for them, and re-layouts: 96.9 us -> 9.36 us
  other arithmetic: 85.2 us -> 0 us
    dot_general x11 -> x0, matrix products: 639 us -> none  [the longest x2 153 us: finish_block(): jnp.einsum('btsd,df->btsf', normed, w_up_blk, preferred_element_type=jnp....]
    pallas_call x0 -> x1, Pallas kernels: none -> 584 us  [run_blocks(): pl.pallas_call(functools.partial(blocks_kernel, (n, heads, hd, local, per...]
    all_to_all x2 -> x0, blocking collectives: 557 us -> none  [the longest x1 320 us: local_run(): mixed_act = lax.all_to_all(mixed_act, 'sp', 2, 1, tiled=True)]
    sub x1 -> x0, matrix products: 84.4 us -> none  [attend(): attn_probs = jax.nn.softmax(scores, axis=-1).astype(jnp.bfloat16)]
    another operation x2 -> x0, local copies, waits for them, and re-layouts: 75.9 us -> none
    sub x1 -> x0, other arithmetic: 42.3 us -> none  [attend(): attn_probs = jax.nn.softmax(scores, axis=-1).astype(jnp.bfloat16)]
    reduce_sum x7 -> x0, other arithmetic: 38.2 us -> none  [the longest x4 24 us: layer_norm(): variance = jnp.mean(centered * centered, axis=-1, keepdims=True)]
    convert_element_type x1 -> x0, local copies, waits for them, and re-layouts: 16.3 us -> none  [finish_block(): return result.astype(jnp.bfloat16)]
where the time goes in v2:
time: 594 us; the launch traced here: 593 us
  Pallas kernels  584 us (98%)
  local copies, waits for them, and re-layouts  9.36 us (2%)
    pallas_call x1, Pallas kernels, run_blocks(): pl.pallas_call(functools.partial(blocks_kernel, (n, heads, hd, local, per...  584 us

profile of v2, /device:TPU:21, one launch (start us, length us, event | category | flops | bytes accessed | tf_op | source)
XLA Modules:
  0.0 593.4 jit_solution(12831229935420729719)
XLA Ops:
  0.0 584.0 %blocks.1 = (bf16[6,96,8,1152]{3,2,1,0:T(8,128)(2,1)}, bf16[16,6,6,8,1152]{4,3,2,1,0:T(8,128)(2,1)}) custom-call(bf16[6,16,6,8,1152]{4,3,2,1,0:T(8,128)(2,1)} %bitcast.8, bf16[4,1152]{1,0:T(4,128)(2,1)} %gain_ref.1, bf16[4,1152]{1,0:T(4,128)(2,1)} %bias_ref.1, bf16[2,3456,1152]{2,1,0:T(8,128)(2,1)} %bitcast.7, bf16[2,1152,1152]{2,1,0:T(8,128)(2,1)} %bitcast.9, ...), custom_call_target="tpu_custom_call" | custom-call | flops 293534171136 | bytes 84934656 | tf_op jit(solution)/shard_map/blocks/pallas_call | solution.py:420
  584.0 9.4 %copy.9 = bf16[1,6,768,1152]{3,2,1,0:T(8,128)(2,1)} copy(bf16[1,6,768,1152]{3,2,1,0:T(8,128)(2,1)} %bitcast.6) | data formatting | bytes 21233664

commit v3 on v2

--- a/solution.py
+++ b/solution.py
@@ -19,6 +19,7 @@
 KB = 128
 RB = 32
 UPB = 512
+DNB = 512
 SLOTS = 3
 NEG = -1e38
 
@@ -49,7 +50,7 @@
 
 def blocks_kernel(cfg, x_hbm, gain_ref, bias_ref, wqkv_hbm, wout_hbm, wup_hbm, wdown_hbm, out_hbm, mid_hbm,
                   wqkv, wout, wup, wdown, xin, xs, a, qkvt, ot, h, nb, nb2, u, y,
-                  s0, s1, p0, p1, m0, m1, l0, l1, wsem, xsem, send_sem, own_sem, mid_sem, out_sem):
+                  s0, s1, p0, p1, m0, m1, l0, l1, qsem, wsem, xsem, send_sem, own_sem, mid_sem, out_sem):
     n, heads, hd, space_units, time_units = cfg
     units = space_units + time_units
     width = heads * hd
@@ -59,6 +60,7 @@
     tok = tiles * rows
     frames = tok // SUB
     groups = rows // SUB
+    pitch = frames + SUB
     lanes = width // LANE
     sbuf, pbuf, mbuf, lbuf = (s0, s1), (p0, p1), (m0, m1), (l0, l1)
     cscale = (hd ** -0.5) * LOG2E
@@ -89,12 +91,19 @@
         pltpu.make_async_copy(part, part, mid_sem.at[t]).wait()
 
     def wcopy(i, layer):
-        src = (wqkv_hbm, wout_hbm, wup_hbm, wdown_hbm)[i]
-        return pltpu.make_async_copy(src.at[layer], (wqkv, wout, wup, wdown)[i], wsem.at[i])
+        src = (wout_hbm, wup_hbm, wdown_hbm)[i]
+        return pltpu.make_async_copy(src.at[layer], (wout, wup, wdown)[i], wsem.at[i])
+
+    def qkv_copy(i, layer):
+        part = aligned(i, width)
+        return pltpu.make_async_copy(wqkv_hbm.at[layer, part], wqkv.at[part], qsem.at[i])
+
+    def qkv_fetch(layer):
+        for i in range(3):
+            qkv_copy(i, layer).start()
 
     xfetch(0, 0)
-    for i in range(4):
-        wcopy(i, 0).start()
+    qkv_fetch(0)
 
     barrier = pltpu.get_barrier_semaphore()
     for k in range(1, n):
@@ -133,7 +142,7 @@
         v = normalize(load_x(slot, t, r0, nr), *par)
         if temporal:
             for c in range(lanes):
-                xs[c, r0:r0 + nr, :] = v[:, c * LANE:(c + 1) * LANE]
+                xs[c, r0 % LANE:r0 % LANE + nr, :] = v[:, c * LANE:(c + 1) * LANE]
         else:
             a[pl.ds(pl.multiple_of(t * rows + r0, nr), nr), :] = v.astype(BF16)
 
@@ -141,7 +150,7 @@
         for p in range(SUB):
             at = pl.ds(pl.multiple_of(p * frames + t * groups + g0, ng), ng)
             for c in range(lanes):
-                a[at, c * LANE:(c + 1) * LANE] = xs[c, pl.ds(g0 * SUB + p, ng, stride=SUB), :].astype(BF16)
+                a[at, c * LANE:(c + 1) * LANE] = xs[c, pl.ds(p, ng, stride=SUB), :].astype(BF16)
 
     def held(c):
         per_buf = tok // LANE
@@ -151,7 +160,7 @@
         if temporal:
             parts = []
             for g in range(r0 // SUB, (r0 + nr) // SUB):
-                at = pl.ds(t * groups + g, SUB, stride=frames)
+                at = pl.ds(t * groups + g, SUB, stride=pitch)
                 parts.append(jnp.concatenate([held(c)[at, :] for c in range(lanes)], axis=1))
             h[t, r0:r0 + nr, :] = (load_x(slot, t, r0, nr) + jnp.concatenate(parts)).astype(BF16)
         dst[r0:r0 + nr, :] = normalize(h[t, r0:r0 + nr, :].astype(F32), *par).astype(BF16)
@@ -271,12 +280,14 @@
             par = params(layer, 0)
 
             def head_norm(t, _):
-                pre_norm(temporal, slot, t, 0, rows, par)
-                if temporal:
-                    spread(t, 0, groups)
+                for r0 in range(0, rows, LANE):
+                    pre_norm(temporal, slot, t, r0, LANE, par)
+                    if temporal:
+                        spread(t, r0 // SUB, LANE // SUB)
                 return 0
             lax.fori_loop(0, tiles, head_norm, 0)
-            wcopy(0, 0).wait()
+            for i in range(3):
+                wcopy(i, layer).start()
 
         pl.when(unit == 0)(lambda: head(False))
 
@@ -294,6 +305,9 @@
             xfetch(unit + 1, 1 - slot)
 
         def qkv_body(i, _):
+            @pl.when(opening)
+            def _():
+                qkv_copy(i, 0).wait()
             r = lax.dot_general(wqkv[aligned(i, width), :], a[...], (((1,), (1,)), ((), ())), preferred_element_type=F32)
             qkvt[pl.ds(heads * i, heads)] = r.reshape(heads, hd, tok).astype(BF16)
             return 0
@@ -301,14 +315,14 @@
 
         @pl.when(closing)
         def _():
-            wcopy(0, 1).start()
+            qkv_fetch(1)
 
         pl.when(layer == 0)(lambda: attention(space_first, space_attend, True))
         pl.when(layer == 1)(lambda: attention(time_first, time_attend, False))
 
         @pl.when(opening)
         def _():
-            wcopy(1, 0).wait()
+            wcopy(0, 0).wait()
 
         par1 = params(layer, 1)
 
@@ -318,8 +332,13 @@
                 r = lax.dot_general(ot[:, cols[b]].astype(BF16), wout[...], (((0,), (0,)), ((), ())),
                                     preferred_element_type=F32)
                 if temporal:
-                    for c in range(lanes):
-                        held(c)[cols[b], :] = r[:, c * LANE:(c + 1) * LANE]
+                    lo = b * QB
+                    while lo < (b + 1) * QB:
+                        p = lo // frames
+                        nr = min((p + 1) * frames, (b + 1) * QB) - lo
+                        for c in range(lanes):
+                            held(c)[lo + p * SUB:lo + p * SUB + nr, :] = r[lo - b * QB:lo - b * QB + nr, c * LANE:(c + 1) * LANE]
+                        lo += nr
                 else:
                     h[b] = (load_x(slot, b, 0, rows) + r).astype(BF16)
                     if b == 0:
@@ -330,14 +349,10 @@
         pl.when(layer == 0)(lambda: project(False))
         pl.when(layer == 1)(lambda: project(True))
 
-        @pl.when(closing)
-        def _():
-            wcopy(1, 1).start()
-
         @pl.when(opening)
         def _():
+            wcopy(1, 0).wait()
             wcopy(2, 0).wait()
-            wcopy(3, 0).wait()
 
         @pl.when(unit == 0)
         def _():
@@ -364,20 +379,32 @@
                 own_wait(ys)
 
             after = jnp.minimum(t + 1, tiles - 1)
-            half = rows // 2
+
+            def now(r0):
+                mid_norm(temporal, nb2, slot, after, r0, piece, par1)
+
+            def later(r0):
+                pre_norm(temporal, 1 - slot, t, r0, piece, par0)
+                if temporal and (r0 + piece) % LANE == 0:
+                    spread(t, (r0 + piece - LANE) // SUB, LANE // SUB)
+
             for i in range(steps):
                 c = i * UPB
                 u[:, c:c + UPB] = gelu(jnp.dot(nb[...], wup[:, c:c + UPB], preferred_element_type=F32)).astype(BF16)
-                r0 = i * piece
-                if r0 < rows:
-                    mid_norm(temporal, nb2, slot, after, r0, piece, par1)
-                    pre_norm(temporal, 1 - slot, t, r0, piece, par0)
-                    if temporal and (r0 + piece) % half == 0:
-                        spread(t, (r0 + piece - half) // SUB, half // SUB)
-            cut = ff - UPB
-            r = jnp.dot(u[:, :cut], wdown[:cut, :], preferred_element_type=F32)
-            r = r + jnp.dot(u[:, cut:], wdown[cut:, :], preferred_element_type=F32)
-            y[ys] = (h[t].astype(F32) + r).astype(BF16).reshape(y.shape[1:])
+                if i * piece < rows:
+                    now(i * piece)
+            cut = ff - 2 * UPB
+            left = list(range(0, rows, piece))
+            for c in range(0, width, DNB):
+                cl = slice(c, min(c + DNB, width))
+                r = jnp.dot(u[:, :cut], wdown[:cut, cl], preferred_element_type=F32)
+                r = r + jnp.dot(u[:, cut:], wdown[cut:, cl], preferred_element_type=F32)
+                y[ys, :, :, :, cl] = (h[t, :, cl].astype(F32) + r).astype(BF16).reshape(y.shape[1:-1] + (-1,))
+                for _ in range(-(-rows // piece * DNB // width)):
+                    if left:
+                        later(left.pop(0))
+            while left:
+                later(left.pop(0))
             nb[...] = nb2[...]
             send(temporal, unit, t, ys)
             return 0
@@ -389,8 +416,6 @@
 
         @pl.when(closing)
         def _():
-            wcopy(2, 1).start()
-            wcopy(3, 1).start()
             for s in range(SLOTS):
                 own_wait(s)
             mid_wait(0)
@@ -426,15 +451,15 @@
         scratch_shapes=[
             pltpu.VMEM((3 * width, width), BF16), pltpu.VMEM((width, width), BF16),
             pltpu.VMEM((width, ff), BF16), pltpu.VMEM((ff, width), BF16),
-            pltpu.VMEM((2, tiles, n, PAIR, SUB, width), BF16), pltpu.VMEM((width // LANE, rows, LANE), F32),
+            pltpu.VMEM((2, tiles, n, PAIR, SUB, width), BF16), pltpu.VMEM((width // LANE, LANE, LANE), F32),
             pltpu.VMEM((tok, width), BF16), pltpu.VMEM((3 * heads, hd, tok), BF16), pltpu.VMEM((width, tok), F32),
             pltpu.VMEM((tiles, rows, width), BF16), pltpu.VMEM((rows, width), BF16), pltpu.VMEM((rows, width), BF16),
             pltpu.VMEM((rows, ff), BF16), pltpu.VMEM((SLOTS, n, PAIR, SUB, width), BF16),
-            pltpu.VMEM((tok // LANE, tok, LANE), F32), pltpu.VMEM((tok // LANE, tok, LANE), F32),
+            pltpu.VMEM((tok // LANE, tok + SUB * SUB + SUB, LANE), F32), pltpu.VMEM((tok // LANE, tok + SUB * SUB + SUB, LANE), F32),
             pltpu.VMEM((tok, tok), BF16), pltpu.VMEM((tok, tok), BF16),
             pltpu.VMEM((8, tok), F32), pltpu.VMEM((8, tok), F32),
             pltpu.VMEM((1, tok), F32), pltpu.VMEM((1, tok), F32),
-            pltpu.SemaphoreType.DMA((4,)), pltpu.SemaphoreType.DMA((2,)), pltpu.SemaphoreType.DMA((SLOTS,)),
+            pltpu.SemaphoreType.DMA((3,)), pltpu.SemaphoreType.DMA((3,)), pltpu.SemaphoreType.DMA((2,)), pltpu.SemaphoreType.DMA((SLOTS,)),
             pltpu.SemaphoreType.DMA((SLOTS,)), pltpu.SemaphoreType.DMA((tiles,)), pltpu.SemaphoreType.DMA,
         ],
         compiler_params=pltpu.CompilerParams(

time: 594 us -> 567 us (0.955)
  Pallas kernels: 584 us -> 556 us
    pallas_call x1, Pallas kernels: 584 us -> 556 us  [run_blocks(): pl.pallas_call(functools.partial(blocks_kernel, (n, heads, hd, local, per...]
where the time goes in v3:
time: 567 us; the launch traced here: 566 us
  Pallas kernels  556 us (98%)
  local copies, waits for them, and re-layouts  9.36 us (2%)
    pallas_call x1, Pallas kernels, run_blocks(): pl.pallas_call(functools.partial(blocks_kernel, (n, heads, hd, local, per...  556 us

profile of v3, /device:TPU:21, one launch (start us, length us, event | category | flops | bytes accessed | tf_op | source)
XLA Modules:
  0.0 565.5 jit_solution(17444051053029629738)
XLA Ops:
  0.0 556.2 %blocks.1 = (bf16[6,96,8,1152]{3,2,1,0:T(8,128)(2,1)}, bf16[16,6,6,8,1152]{4,3,2,1,0:T(8,128)(2,1)}) custom-call(bf16[6,16,6,8,1152]{4,3,2,1,0:T(8,128)(2,1)} %bitcast.8, bf16[4,1152]{1,0:T(4,128)(2,1)} %gain_ref.1, bf16[4,1152]{1,0:T(4,128)(2,1)} %bias_ref.1, bf16[2,3456,1152]{2,1,0:T(8,128)(2,1)} %bitcast.7, bf16[2,1152,1152]{2,1,0:T(8,128)(2,1)} %bitcast.9, ...), custom_call_target="tpu_custom_call" | custom-call | flops 293534171136 | bytes 84934656 | tf_op jit(solution)/shard_map/blocks/pallas_call | solution.py:445
  556.2 9.4 %copy.9 = bf16[1,6,768,1152]{3,2,1,0:T(8,128)(2,1)} copy(bf16[1,6,768,1152]{3,2,1,0:T(8,128)(2,1)} %bitcast.6) | data formatting | bytes 21233664
